TPU v7x, 128 devices: a whole 4x4x4 slice. The times are simulated.
128 devices in a mesh: fsdp: 8 (over z_lo, x), tp: 16 (over y, z_hi, core).
Axes of the slice: x: 4, y: 4, z: 4 (z_hi: 2, z_lo: 2; z = z_hi * 2 + z_lo), core: 2. Of those that a mesh axis runs over, the one named last changes fastest.
Arguments:
- ref_gate: bfloat16 [6144, 11008], P('fsdp', 'tp'), may hold values from -6 to 6
- ref_up: bfloat16 [6144, 11008], P('fsdp', 'tp'), may hold values from -6 to 6
- ref_residual: bfloat16 [6144, 4096], P('fsdp', 'tp'), may hold values from -6 to 6
- ref_modality: int32 [6144], P('fsdp'), may hold values 0 or 1
- ref_down_text: bfloat16 [4096, 11008], P('fsdp', 'tp'), may hold values from -0.0546875 to 0.0546875
- ref_down_image: bfloat16 [4096, 11008], P('fsdp', 'tp'), may hold values from -0.0546875 to 0.0546875
- pol_gate: bfloat16 [6144, 11008], P('fsdp', 'tp'), may hold values from -6 to 6
- pol_up: bfloat16 [6144, 11008], P('fsdp', 'tp'), may hold values from -6 to 6
- pol_modality: int32 [6144], P('fsdp'), may hold values 0 or 1
- pol_segment: int32 [6144], P('fsdp'), may hold values from 0 to 11, never falling along the last dimension, each value on 1 to 768 neighbouring positions
- pair_margin: float32 [6], replicated, may hold values from -30 to 30
- token_cotangent: bfloat16 [6144, 4096], P('fsdp', 'tp'), may hold values from -24 to 24
- pol_down_text: bfloat16 [4096, 11008], P('fsdp', 'tp'), may hold values from -0.0546875 to 0.0546875
- pol_down_image: bfloat16 [4096, 11008], P('fsdp', 'tp'), may hold values from -0.0546875 to 0.0546875
Outputs:
- ref_out: bfloat16 [6144, 4096], P('fsdp', 'tp')
- grad_gate: bfloat16 [6144, 11008], P('fsdp', 'tp')
- grad_up: bfloat16 [6144, 11008], P('fsdp', 'tp')
- grad_down_text: float32 [4096, 11008], P('fsdp', 'tp')
- grad_down_image: float32 [4096, 11008], P('fsdp', 'tp')
Inputs may be any that keep to these rules, and one draw needn't show every extreme that they name: `ref_modality`: 0 marks a text token, 1 an image token. `pol_modality`: 0 marks a text token, 1 an image token. `pol_segment`: response numbers never fall along the tokens; responses 2p and 2p + 1 are the chosen and the rejected response of pair p; every response has at least one token.
All inputs are finite; a program needn't handle non-finite values. No bound on the sum of `ref_modality` or of `pol_modality` on one device may be relied on, other than what follows from the above.
Results may differ from a plain program's by a relative error of at most 0.015.
Values may be sent and summed in bfloat16 or wider, within the bound.
No kernel may reach another device: no remote copies, remote signals or barrier semaphores. Data moves between devices by JAX's collectives and lax.ppermute only.
A program may use at most 128 MiB of HBM per device.

v0:
```python
import jax
import jax.numpy as jnp
from jax import lax
from jax.sharding import PartitionSpec as P

dpo_beta = 0.1


def sent_together(arrays, axis, dim, along):
    ends, at = ([], 0)
    for a in arrays[:-1]:
        at += a.shape[along]
        ends.append(at)
    both = jnp.concatenate(arrays, axis=along)
    return tuple(jnp.split(lax.all_gather(both, axis, axis=dim, tiled=True), ends, axis=along))


def split_hidden(gate, up, modality):
    gate_f = gate.astype(jnp.float32)
    up_f = up.astype(jnp.float32)
    sig = jax.nn.sigmoid(gate_f)
    act = gate_f * sig
    hidden = (act * up_f).astype(jnp.bfloat16)
    image = (modality == 1)[:, None]
    zero = jnp.zeros_like(hidden)
    return (jnp.where(image, zero, hidden), jnp.where(image, hidden, zero), gate_f, up_f, sig, act)


def forward_term(left_text, left_image, right_text, right_image):
    contract = (((1,), (1,)), ((), ()))
    part = lax.dot_general(left_text, right_text, contract, preferred_element_type=jnp.float32)
    return part + lax.dot_general(
        left_image, right_image, contract, preferred_element_type=jnp.float32
    )


def backward_term(left_text, left_image, right_text, right_image):
    part = jnp.dot(left_text, right_text, preferred_element_type=jnp.float32)
    return part + jnp.dot(left_image, right_image, preferred_element_type=jnp.float32)


def per_device(
    ref_gate,
    ref_up,
    ref_residual,
    ref_modality,
    ref_down_text,
    ref_down_image,
    pol_gate,
    pol_up,
    pol_modality,
    pol_segment,
    pair_margin,
    token_cotangent,
    pol_down_text,
    pol_down_image,
):
    ref_text, ref_image, _, _, _, _ = split_hidden(ref_gate, ref_up, ref_modality)
    pol_text, pol_image, gate_f, up_f, sig, act = split_hidden(pol_gate, pol_up, pol_modality)
    seg_ids = jnp.arange(2 * pair_margin.shape[0], dtype=jnp.int32)
    pair_weight = dpo_beta * jax.nn.sigmoid(-dpo_beta * pair_margin)
    table = jnp.repeat(pair_weight, 2) * jnp.where(seg_ids % 2 == 0, -1.0, 1.0).astype(jnp.float32)
    coef = jnp.sum(
        jnp.where(pol_segment[:, None] == seg_ids[None, :], table[None, :], jnp.float32(0.0)),
        axis=1,
    )
    local_cot = (coef[:, None] * token_cotangent.astype(jnp.float32)).astype(jnp.bfloat16)
    full_cot = lax.all_gather(local_cot, "tp", axis=1, tiled=True)
    image_p = (pol_modality == 1)[:, None]
    zero_cot = jnp.zeros_like(full_cot)
    cot_text = jnp.where(image_p, zero_cot, full_cot)
    cot_image = jnp.where(image_p, full_cot, zero_cot)
    whole_rt, whole_ri, whole_pt, whole_pi = sent_together(
        (ref_down_text, ref_down_image, pol_down_text, pol_down_image), "fsdp", 0, 1
    )
    terms = forward_term(ref_text, ref_image, whole_rt, whole_ri)
    d_hidden = backward_term(cot_text, cot_image, whole_pt, whole_pi)
    summed = lax.psum_scatter(
        terms.astype(jnp.bfloat16), "tp", scatter_dimension=1, tiled=True
    ).astype(jnp.float32)
    ref_out = (summed + ref_residual.astype(jnp.float32)).astype(jnp.bfloat16)
    grad_gate = (d_hidden * up_f * sig * (1.0 + gate_f * (1.0 - sig))).astype(jnp.bfloat16)
    grad_up = (d_hidden * act).astype(jnp.bfloat16)
    width = pol_down_text.shape[1]
    over_rows = (((0,), (0,)), ((), ()))
    term_text = lax.dot_general(cot_text, pol_text, over_rows, preferred_element_type=jnp.float32)
    term_image = lax.dot_general(
        cot_image, pol_image, over_rows, preferred_element_type=jnp.float32
    )
    grads = lax.psum_scatter(
        jnp.concatenate([term_text, term_image], axis=1).astype(jnp.bfloat16),
        "fsdp",
        scatter_dimension=0,
        tiled=True,
    ).astype(jnp.float32)
    return (ref_out, grad_gate, grad_up, grads[:, :width], grads[:, width:])


def solution(mesh):
    in_specs = (
        P("fsdp", "tp"),
        P("fsdp", "tp"),
        P("fsdp", "tp"),
        P("fsdp"),
        P("fsdp", "tp"),
        P("fsdp", "tp"),
        P("fsdp", "tp"),
        P("fsdp", "tp"),
        P("fsdp"),
        P("fsdp"),
        P(),
        P("fsdp", "tp"),
        P("fsdp", "tp"),
        P("fsdp", "tp"),
    )
    out_specs = (
        P("fsdp", "tp"),
        P("fsdp", "tp"),
        P("fsdp", "tp"),
        P("fsdp", "tp"),
        P("fsdp", "tp"),
    )
    return jax.shard_map(
        per_device, mesh=mesh, in_specs=in_specs, out_specs=out_specs, check_vma=False
    )
```

profile of v0, /device:TPU:0, one launch (start us, length us, event | category | flops | bytes accessed | tf_op | source)
XLA Modules:
  0.0 529.0 jit_solution(288210245870872746)
XLA Ops:
  7.2 0.0 all-gather.5.cloned.1.call-start
  7.2 0.7 divide_multiply_fusion
  7.9 0.1 broadcast_in_dim.66
  7.9 0.1 reshape.33
  8.0 0.8 select_reduce_fusion
  8.8 1.9 multiply_convert_fusion.1
  10.7 0.0 all-gather.5.cloned.1.call-update
  10.8 0.0 all-gather.3.cloned.1.call-start
  10.8 3.0 pad_maximum_fusion.1
  13.8 0.0 copy-start.1
  13.8 0.0 copy-start.6
  13.8 0.0 copy-start.7
  13.8 0.0 all-gather.3.cloned.1.call-update
  13.9 0.0 reduce-scatter.5.cloned.1.call-start
  13.9 0.6 copy-done.1
  14.5 67.7 %all-gather.5.cloned.1.call-done = bf16[768,4096]{1,0:T(8,128)(2,1)} async-done(((bf16[768,256]{1,0:T(8,128)(2,1)}), bf16[768,4096]{1,0:T(8,128)(2,1)}) %all-gather.5.cloned.1.call-update) | async-done | bytes 6291472 | tf_op jit(solution)/shard_map/all_gather | solution.py:68
  82.2 0.0 copy-done.6
  82.2 0.0 copy-done.7
  82.2 0.0 copy-start.3
  82.2 8.2 %convolution_convert_fusion = bf16[4096,688]{0,1:T(8,128)(2,1)S(1)} fusion(bf16[768,4096]{1,0:T(8,128)(2,1)} %all-gather.5.cloned.1.call-done, pred[768]{0:T(1024)(128)(4,1)S(1)} %broadcast_compare_fusion, bf16[768,688]{0,1:T(8,128)(2,1)S(1)} %copy-done.6, bf16[768,688]{0,1:T(8,128)(2,1)S(1)} %copy-done.7), kind=kOutput, calls=%fused_computation.2 | convolution fusion | flops 4339240960 | bytes 14041856 | tf_op jit(solution)/shard_map/dot_general | solution.py:87
  90.4 0.0 copy-done.3
  90.4 5.3 %convolution_convert_fusion.1 = bf16[4096,688]{0,1:T(8,128)(2,1)S(1)} fusion(bf16[768,4096]{1,0:T(8,128)(2,1)S(1)} %copy-done.3, pred[768]{0:T(1024)(128)(4,1)S(1)} %broadcast_compare_fusion, bf16[768,688]{0,1:T(8,128)(2,1)S(1)} %copy-done.6, bf16[768,688]{0,1:T(8,128)(2,1)S(1)} %copy-done.7), kind=kOutput, calls=%fused_computation.3 | convolution fusion | flops 4339240960 | bytes 14041856 | tf_op jit(solution)/shard_map/dot_general | solution.py:86
  95.7 10.4 %pad_maximum_fusion = bf16[4096,1376]{0,1:T(8,128)(2,1)} fusion(bf16[4096,688]{0,1:T(8,128)(2,1)S(1)} %convolution_convert_fusion, bf16[4096,688]{0,1:T(8,128)(2,1)S(1)} %convolution_convert_fusion.1), kind=kLoop, calls=%fused_computation.1 | loop fusion | flops 22544384 | bytes 22544384 | tf_op jit(solution)/shard_map/concatenate | solution.py:91
  106.1 0.0 copy-start.2
  106.1 0.0 copy-start.4
  106.2 0.0 copy-start.5
  106.2 0.0 reduce-scatter.5.cloned.1.call-update
  106.2 0.2 reduce-scatter.3.cloned.1.call-start
  106.4 0.4 copy-done.2
  106.8 200.0 %all-gather.3.cloned.1.call-done = bf16[4096,2752]{0,1:T(8,128)(2,1)} async-done(((bf16[512,2752]{0,1:T(8,128)(2,1)}), bf16[4096,2752]{0,1:T(8,128)(2,1)}) %all-gather.3.cloned.1.call-update) | async-done | bytes 22544400 | tf_op jit(solution)/shard_map/all_gather | solution.py:15
  306.8 0.0 copy-done.4
  306.8 0.0 copy-done.5
  306.8 7.6 %fusion.5 = f32[768,4096]{1,0:T(8,128)S(1)} fusion(bf16[4096,2752]{0,1:T(8,128)(2,1)} %all-gather.3.cloned.1.call-done, pred[768]{0:T(1024)(128)(4,1)S(1)} %broadcast_compare_fusion.1, bf16[768,688]{0,1:T(8,128)(2,1)S(1)} %copy-done.4, bf16[768,688]{0,1:T(8,128)(2,1)S(1)} %copy-done.5), kind=kOutput, calls=%fused_computation.11 | convolution fusion | flops 4333277184 | bytes 20333312 | tf_op jit(solution)/shard_map/dot_general | solution.py:31
  314.4 10.6 %add_convert_fusion = bf16[768,4096]{1,0:T(8,128)(2,1)} fusion(f32[768,4096]{1,0:T(8,128)S(1)} %fusion.5, bf16[4096,2752]{0,1:T(8,128)(2,1)} %all-gather.3.cloned.1.call-done, pred[768]{0:T(1024)(128)(4,1)S(1)} %broadcast_compare_fusion.1, bf16[768,688]{0,1:T(8,128)(2,1)S(1)} %copy-done.4, bf16[768,688]{0,1:T(8,128)(2,1)S(1)} %copy-done.5), kind=kOutput, calls=%fused_computation | convolution fusion | flops 4339568640 | bytes 26624768 | tf_op jit(solution)/shard_map/dot_general | solution.py:32
  325.1 0.0 reduce-scatter.3.cloned.1.call-update
  325.1 102.9 %reduce-scatter.5.cloned.1.call-done = bf16[512,1376]{0,1:T(8,128)(2,1)} async-done(((bf16[4096,1376]{0,1:T(8,128)(2,1)}), bf16[512,1376]{0,1:T(8,128)(2,1)}) %reduce-scatter.5.cloned.1.call-update) | async-done | bytes 1409040 | tf_op jit(solution)/shard_map/reduce_scatter | solution.py:90
  428.0 0.0 slice-start
  428.0 3.4 fusion.46
  431.4 0.0 copy-start.8
  431.4 8.8 %fusion = f32[768,688]{0,1:T(8,128)S(1)} fusion(bf16[4096,2752]{0,1:T(8,128)(2,1)} %all-gather.3.cloned.1.call-done, bf16[768,4096]{1,0:T(8,128)(2,1)} %all-gather.5.cloned.1.call-done, pred[768]{0:T(1024)(128)(4,1)S(1)} %broadcast_compare_fusion), kind=kOutput, calls=%fused_computation.6 | convolution fusion | flops 4331667456 | bytes 14041856 | tf_op jit(solution)/shard_map/dot_general | solution.py:39
  440.2 0.0 slice-done
  440.2 0.0 slice-done.1
  440.2 0.0 copy-done.8
  440.2 0.0 copy-start
  440.3 9.8 %multiply_convert_fusion = (bf16[768,688]{0,1:T(8,128)(2,1)}, bf16[768,688]{0,1:T(8,128)(2,1)}) fusion(bf16[768,688]{0,1:T(8,128)(2,1)S(1)} %copy-done.8, bf16[768,688]{0,1:T(8,128)(2,1)S(1)} %copy-done.6, f32[768,688]{0,1:T(8,128)S(1)} %fusion, bf16[4096,2752]{0,1:T(8,128)(2,1)} %all-gather.3.cloned.1.call-done, bf16[768,4096]{1,0:T(8,128)(2,1)S(1)} %bitcast.1, ...), kind=kOutput, calls=%fused_computation.33 | convolution fusion | flops 4340121600 | bytes 18268928 | tf_op jit(solution)/shard_map/dot_general | solution.py:38
  450.0 70.6 %reduce-scatter.3.cloned.1.call-done = bf16[768,256]{1,0:T(8,128)(2,1)} async-done(((bf16[768,4096]{1,0:T(8,128)(2,1)}), bf16[768,256]{1,0:T(8,128)(2,1)}) %reduce-scatter.3.cloned.1.call-update) | async-done | bytes 393232 | tf_op jit(solution)/shard_map/reduce_scatter | solution.py:78
  520.6 0.0 copy-done
  520.6 1.8 add_convert_fusion.1
  (5 shorter events, 0.0 us)
Async XLA Ops:
  7.2 75.0 %all-gather.5.cloned.1.call-start = ((), (), s32[]{:S(2)}) async-start(), calls=%async_computation.4 | async-start | bytes 6684672 | tf_op jit(solution)/shard_map/all_gather | solution.py:68
  10.8 296.1 %all-gather.3.cloned.1.call-start = ((), (), s32[]{:S(2)}) async-start(), calls=%async_computation.2 | async-start | bytes 25362432 | tf_op jit(solution)/shard_map/all_gather | solution.py:15
  13.8 0.7 copy-start.1
  13.8 68.4 %copy-start.6 = (bf16[768,688]{0,1:T(8,128)(2,1)S(1)}, bf16[768,688]{0,1:T(8,128)(2,1)}, u32[]{:S(2)}) copy-start(bf16[768,688]{0,1:T(8,128)(2,1)} %param.21) | copy-start | bytes 3170308
  13.8 68.4 %copy-start.7 = (bf16[768,688]{0,1:T(8,128)(2,1)S(1)}, bf16[768,688]{0,1:T(8,128)(2,1)}, u32[]{:S(2)}) copy-start(bf16[768,688]{0,1:T(8,128)(2,1)} %param.20) | copy-start | bytes 3170308
  13.9 414.1 %reduce-scatter.5.cloned.1.call-start = ((), (), s32[]{:S(2)}) async-start(), calls=%async_computation.5 | async-start | bytes 12681216 | tf_op jit(solution)/shard_map/reduce_scatter | solution.py:90
  82.2 8.2 %copy-start.3 = (bf16[768,4096]{1,0:T(8,128)(2,1)S(1)}, bf16[768,4096]{1,0:T(8,128)(2,1)}, u32[]{:S(2)}) copy-start(bf16[768,4096]{1,0:T(8,128)(2,1)} %all-gather.5.cloned.1.call-done) | copy-start | bytes 18874372
  106.1 0.7 copy-start.2
  106.1 200.7 %copy-start.4 = (bf16[768,688]{0,1:T(8,128)(2,1)S(1)}, bf16[768,688]{0,1:T(8,128)(2,1)}, u32[]{:S(2)}) copy-start(bf16[768,688]{0,1:T(8,128)(2,1)} %param.15) | copy-start | bytes 3170308
  106.2 200.7 %copy-start.5 = (bf16[768,688]{0,1:T(8,128)(2,1)S(1)}, bf16[768,688]{0,1:T(8,128)(2,1)}, u32[]{:S(2)}) copy-start(bf16[768,688]{0,1:T(8,128)(2,1)} %param.14) | copy-start | bytes 3170308
  106.2 414.4 %reduce-scatter.3.cloned.1.call-start = ((), (), s32[]{:S(2)}) async-start(), calls=%async_computation.3 | async-start | bytes 6684672 | tf_op jit(solution)/shard_map/reduce_scatter | solution.py:78
  428.0 12.2 %slice-start = ((s8[6291456]{0:T(1024)(128)(4,1)}), s8[4194304]{0:T(1024)(128)(4,1)S(1)}, s32[]{:S(2)}) async-start(s8[6291456]{0:T(1024)(128)(4,1)} %bitcast), calls=%async_computation.6 | async-start | bytes 8388608
  431.4 8.8 %slice-start.1 = ((s8[6291456]{0:T(1024)(128)(4,1)}), s8[2097152]{0:T(1024)(128)(4,1)S(1)}, s32[]{:S(2)}) async-start(s8[6291456]{0:T(1024)(128)(4,1)} %bitcast), calls=%async_computation.7 | async-start | bytes 4194304
  431.4 8.8 %copy-start.8 = (bf16[768,688]{0,1:T(8,128)(2,1)S(1)}, bf16[768,688]{0,1:T(8,128)(2,1)}, u32[]{:S(2)}) copy-start(bf16[768,688]{0,1:T(8,128)(2,1)} %param.20) | copy-start | bytes 3170308
  440.2 80.4 %copy-start = (bf16[768,256]{1,0:T(8,128)(2,1)S(1)}, bf16[768,256]{1,0:T(8,128)(2,1)}, u32[]{:S(2)}) copy-start(bf16[768,256]{1,0:T(8,128)(2,1)} %param.16) | copy-start | bytes 1179652
Sparse Core Ops, SparseCore 0:
  10.9 71.2 all-gather.4
  83.9 222.9 all-gather.2
  309.2 118.6 reduce-scatter.4
  432.0 88.5 reduce-scatter.2
where the time goes:
time: 529 us
  waiting for transfers between devices  441 us (83%)
  matrix products  50.3 us (10%)
  other arithmetic  18.6 us (4%)
  between operations  13.9 us (3%)
    all_gather x1, waiting for transfers between devices, sent_together(): lax.all_gather(both, axis, axis=dim, tiled=True)  200 us
    reduce_scatter x1, waiting for transfers between devices, per_device(): lax.psum_scatter(jnp.concatenate([term_text, term_image], axis=1).astype(...  103 us
    reduce_scatter x1, waiting for transfers between devices, per_device(): lax.psum_scatter(terms.astype(jnp.bfloat16), 'tp', scatter_dimension=1, t...  70.6 us
    all_gather x1, waiting for transfers between devices, per_device(): full_cot = lax.all_gather(local_cot, 'tp', axis=1, tiled=True)  67.7 us
    dot_general x1, matrix products, forward_term(): lax.dot_general(left_image, right_image, contract, preferred_element_type...  10.6 us
  transfers between devices with their start and end apart: 4, of which 4 were waited for; matrix products, arithmetic and copies ran while one was open for 13% of the time, Pallas kernels for 0%

commit v1 on v0

v1 whole, which is shorter than its diff:
```python
import jax
import jax.numpy as jnp
from jax import lax
from jax.experimental import pallas as pl
from jax.experimental.pallas import tpu as pltpu
from jax.sharding import PartitionSpec as P

dpo_beta = 0.1


F32 = jnp.float32
VMEM_BYTES = 63 * 2**20
BF16 = jnp.bfloat16
ANY = pl.BlockSpec(memory_space=pl.ANY)
SMEM = pl.BlockSpec(memory_space=pltpu.SMEM)
VMEM = pl.BlockSpec(memory_space=pltpu.VMEM)

NX, NY, N_FSDP, N_TP = 4, 4, 8, 16


def move_x(s):
    return [(f, (f // NX) * NX + (f % NX + s) % NX) for f in range(N_FSDP)]


def move_y(s):
    return [(k, ((k // 4 + s) % NY) * 4 + k % 4) for k in range(N_TP)]


SWAP_ZLO = [(f, f ^ NX) for f in range(N_FSDP)]
SWAP_ZHI = [(k, k ^ 2) for k in range(N_TP)]
SWAP_CORE = [(k, k ^ 1) for k in range(N_TP)]


def tile_pairs():
    pairs = []
    for f in range(N_FSDP):
        for k in range(N_TP):
            zl, xs = divmod(f, NX)
            ys, zhs, c = k // 4, (k // 2) % 2, k % 2
            x = (ys % 2) * 2 + zhs
            y = (xs - x) % NX
            zh = (ys // 2) ^ zl
            pairs.append((f * N_TP + k, (zl * NX + x) * N_TP + y * 4 + zh * 2 + c))
    return pairs


TO_GROUP = tile_pairs()
FROM_GROUP = [(b, a) for a, b in TO_GROUP]


def pad_up(n, m):
    return -(-n // m) * m


def cost(flops, nbytes):
    return pl.CostEstimate(flops=int(flops), bytes_accessed=int(nbytes), transcendentals=0)


def load_cot(me_ref, tiles, cot, sems):
    y, zh, c = me_ref[0], me_ref[1], me_ref[2]
    width = tiles[0].shape[1]
    copies = []
    for i, t in enumerate(tiles):
        r, q, h = i // 4, (i // 2) % 2, i % 2
        col = pl.multiple_of((c ^ h) * width, width)
        dst = cot.at[(y + r) % NY, zh ^ q, :, pl.ds(col, width)]
        cp = pltpu.make_async_copy(t, dst, sems.at[0])
        cp.start()
        copies.append(cp)
    return copies


def load_hidden(blocks, raw, sems):
    own, left, opp_a, opp_b, right = blocks
    split = opp_a.shape[0]
    copies = []
    for s, at, src in ((0, 0, own), (1, 0, left), (2, 0, opp_a), (2, split, opp_b), (3, 0, right)):
        cp = pltpu.make_async_copy(src, raw.at[s, pl.ds(at, src.shape[0]), :], sems.at[1 + s])
        cp.start()
        copies.append(cp)
    return copies


def dw_kernel(me_ref, mod_ref, *refs):
    tiles, halves = refs[:16], refs[16:21]
    outs = refs[21:25]
    cot, raw, acc, send, sems = refs[25:]
    waits = load_cot(me_ref, tiles, cot, sems)
    hw = load_hidden(halves, raw, sems)
    acc[...] = jnp.zeros_like(acc)
    for w in waits + hw:
        w.wait()

    def body(s, carry):
        image = mod_ref[pl.ds(s, 1), :] == 1
        h = raw[s]
        zero = jnp.zeros_like(h)
        for m in range(2):
            hm = jnp.where(image, zero, h) if m == 0 else jnp.where(image, h, zero)
            for q in range(2):
                acc[m, q] += jnp.dot(hm, cot[s, q], preferred_element_type=F32)
        return carry

    lax.fori_loop(0, NX, body, 0)
    copies = []
    for m in range(2):
        send[m] = acc[m, 1].astype(BF16)
        copies.append(pltpu.make_async_copy(acc.at[m, 0], outs[m], sems.at[5]))
        copies.append(pltpu.make_async_copy(send.at[m], outs[2 + m], sems.at[6]))
    for cp in copies:
        cp.start()
    for cp in copies:
        cp.wait()


def run_dw(me, mod, tiles, halves):
    units = halves[0].shape[0]
    tokens = halves[0].shape[1]
    rows = 2 * tiles[0].shape[1]
    return pl.pallas_call(
        dw_kernel,
        name="dw",
        out_shape=[jax.ShapeDtypeStruct((units, rows), F32)] * 2
        + [jax.ShapeDtypeStruct((units, rows), BF16)] * 2,
        in_specs=[SMEM, VMEM] + [ANY] * 21,
        out_specs=[ANY] * 4,
        scratch_shapes=[
            pltpu.VMEM((NX, 2, tokens, rows), BF16),
            pltpu.VMEM((NX, units, tokens), BF16),
            pltpu.VMEM((2, 2, units, rows), F32),
            pltpu.VMEM((2, units, rows), BF16),
            pltpu.SemaphoreType.DMA((7,)),
        ],
        cost_estimate=cost(2 * NX * tokens * rows * units * 4, 20e6),
        compiler_params=pltpu.CompilerParams(vmem_limit_bytes=VMEM_BYTES),
    )(me, mod, *tiles, *halves)


def dh_kernel(me_ref, mod_ref, *refs):
    tiles, ws = refs[:16], refs[16:20]
    outs = refs[20:28]
    cot, w, part, own, sems = refs[28:]
    waits = load_cot(me_ref, tiles, cot, sems)
    for m in range(2):
        for q in range(2):
            cp = pltpu.make_async_copy(ws[2 * q + m], w.at[m, q], sems.at[1])
            cp.start()
            waits.append(cp)
    for cp in waits:
        cp.wait()
    half = part.shape[-1]
    nt = (((1,), (1,)), ((), ()))

    def body(i, carry):
        s = (i + 2) % NX
        for j in range(2):
            both = []
            for m in range(2):
                p = None
                for q in range(2):
                    t = lax.dot_general(
                        w[m, q], cot[s, q, pl.ds(j * half, half), :], nt, preferred_element_type=F32
                    )
                    p = t if p is None else p + t
                both.append(p)
            image = mod_ref[pl.ds(s, 1), pl.ds(j * half, half)] == 1
            dh = jnp.where(image, both[1], both[0])
            part[s, j] = dh.astype(BF16)

            @pl.when(s == 0)
            def _():
                own[j] = dh

        return carry

    lax.fori_loop(0, NX, body, 0)
    copies = []
    for j in range(2):
        copies.append(pltpu.make_async_copy(own.at[j], outs[j], sems.at[2]))
        for s in range(1, NX):
            copies.append(pltpu.make_async_copy(part.at[s, j], outs[2 * s + j], sems.at[3]))
    for cp in copies:
        cp.start()
    for cp in copies:
        cp.wait()


def run_dh(me, mod, tiles, ws):
    units, rows = ws[0].shape
    tokens = tiles[0].shape[0]
    half = tokens // 2
    return pl.pallas_call(
        dh_kernel,
        name="dh",
        out_shape=[jax.ShapeDtypeStruct((units, half), F32)] * 2
        + [jax.ShapeDtypeStruct((units, half), BF16)] * 6,
        in_specs=[SMEM, VMEM] + [ANY] * 20,
        out_specs=[ANY] * 8,
        scratch_shapes=[
            pltpu.VMEM((NX, 2, tokens, rows), BF16),
            pltpu.VMEM((2, 2, units, rows), BF16),
            pltpu.VMEM((NX, 2, units, half), BF16),
            pltpu.VMEM((2, units, half), F32),
            pltpu.SemaphoreType.DMA((4,)),
        ],
        cost_estimate=cost(2 * NX * tokens * rows * units * 4, 16e6),
        compiler_params=pltpu.CompilerParams(vmem_limit_bytes=VMEM_BYTES),
    )(me, mod, *tiles, *ws)


def fwd_kernel(me_ref, mod_ref, *refs):
    halves, ws = refs[:5], refs[5:9]
    outs = refs[9:17]
    raw, wraw, wt, out, sems = refs[17:]
    y, zh, c = me_ref[0], me_ref[1], me_ref[2]
    units, padded = ws[0].shape[0], raw.shape[1]
    waits = []
    for m in range(2):
        for q in range(2):
            cp = pltpu.make_async_copy(ws[2 * q + m], wraw.at[m, q, pl.ds(0, units), :], sems.at[0])
            cp.start()
            waits.append(cp)
    waits += load_hidden(halves, raw, sems)
    if padded > units:
        raw[:, units:, :] = jnp.zeros((NX, padded - units, raw.shape[2]), BF16)
        wraw[:, :, units:, :] = jnp.zeros((2, 2, padded - units, wraw.shape[3]), BF16)
    for cp in waits:
        cp.wait()
    for m in range(2):
        for q in range(2):
            wt[m, q] = wraw[m, q].T
    block = out.shape[3]

    def body(s, carry):
        image = mod_ref[pl.ds(s, 1), :] == 1
        h = raw[s]
        zero = jnp.zeros_like(h)
        text, img = jnp.where(image, zero, h), jnp.where(image, h, zero)
        for q in range(2):
            for k in range(2):
                at = pl.ds(k * block, block)
                p = jnp.dot(wt[0, q, at, :], text, preferred_element_type=F32)
                p = p + jnp.dot(wt[1, q, at, :], img, preferred_element_type=F32)
                out[s, q, k] = p.astype(BF16)
        return carry

    lax.fori_loop(0, NX, body, 0)
    copies = []
    for r in range(NY):
        for h in range(2):
            for q in range(2):
                src = out.at[(y + r) % NY, zh ^ q, c ^ h]
                copies.append(pltpu.make_async_copy(src, outs[2 * r + h].at[q], sems.at[5]))
    for cp in copies:
        cp.start()
    for cp in copies:
        cp.wait()


def run_fwd(me, mod, halves, ws):
    units, rows = ws[0].shape
    tokens = halves[0].shape[1]
    block, padded = rows // 2, pad_up(units, 256)
    return pl.pallas_call(
        fwd_kernel,
        name="fwd",
        out_shape=[jax.ShapeDtypeStruct((2, block, tokens), BF16)] * 8,
        in_specs=[SMEM, VMEM] + [ANY] * 9,
        out_specs=[ANY] * 8,
        scratch_shapes=[
            pltpu.VMEM((NX, padded, tokens), BF16),
            pltpu.VMEM((2, 2, padded, rows), BF16),
            pltpu.VMEM((2, 2, rows, padded), BF16),
            pltpu.VMEM((NX, 2, 2, block, tokens), BF16),
            pltpu.SemaphoreType.DMA((6,)),
        ],
        cost_estimate=cost(2 * NX * tokens * rows * units * 4, 14e6),
        compiler_params=pltpu.CompilerParams(vmem_limit_bytes=VMEM_BYTES),
    )(me, mod, *halves, *ws)


def add(*terms):
    total = terms[0].astype(F32)
    for t in terms[1:]:
        total = total + t.astype(F32)
    return total.astype(BF16)


def gather_x(own):
    split = pad_up(own.shape[0] // 2, 16)
    right = lax.ppermute(own, "fsdp", move_x(1))
    left = lax.ppermute(own, "fsdp", move_x(-1))
    opp_a = lax.ppermute(right[:split], "fsdp", move_x(1))
    opp_b = lax.ppermute(left[split:], "fsdp", move_x(-1))
    return [own, left, opp_a, opp_b, right]


def hidden_of(gate_t, up_t):
    gate_f, up_f = gate_t.astype(F32), up_t.astype(F32)
    return (gate_f * jax.nn.sigmoid(gate_f) * up_f).astype(BF16)


def per_device(
    ref_gate,
    ref_up,
    ref_residual,
    ref_modality,
    ref_down_text,
    ref_down_image,
    pol_gate,
    pol_up,
    pol_modality,
    pol_segment,
    pair_margin,
    token_cotangent,
    pol_down_text,
    pol_down_image,
):
    k = lax.axis_index("tp")
    me = jnp.stack([k // 4, (k // 2) % 2, k % 2]).astype(jnp.int32)

    seg_ids = jnp.arange(2 * pair_margin.shape[0], dtype=jnp.int32)
    pair_weight = dpo_beta * jax.nn.sigmoid(-dpo_beta * pair_margin)
    table = jnp.repeat(pair_weight, 2) * jnp.where(seg_ids % 2 == 0, -1.0, 1.0).astype(F32)
    coef = jnp.sum(
        jnp.where(pol_segment[:, None] == seg_ids[None, :], table[None, :], F32(0.0)), axis=1
    )
    cot = (coef[:, None] * token_cotangent.astype(F32)).astype(BF16)
    t0 = lax.ppermute(cot, ("fsdp", "tp"), TO_GROUP)

    mods = jnp.stack([ref_modality, pol_modality])
    mod_r = lax.ppermute(mods, "fsdp", move_x(1))
    mod_l = lax.ppermute(mods, "fsdp", move_x(-1))
    mod_o = lax.ppermute(mod_r, "fsdp", move_x(1))
    mods = jnp.stack([mods, mod_l, mod_o, mod_r], axis=1)

    pol_gate_t, pol_up_t = pol_gate.T, pol_up.T
    ref_h = gather_x(hidden_of(ref_gate.T, ref_up.T))
    pol_h = gather_x(hidden_of(pol_gate_t, pol_up_t))

    def both_rows(text, image):
        own = (text.T, image.T)
        return own + tuple(lax.ppermute(w, "fsdp", SWAP_ZLO) for w in own)

    ref_w = both_rows(ref_down_text, ref_down_image)
    pol_w = both_rows(pol_down_text, pol_down_image)

    t1 = lax.ppermute(t0, "tp", SWAP_ZHI)
    r0, l0 = lax.ppermute(t0, "tp", move_y(1)), lax.ppermute(t0, "tp", move_y(-1))
    r1, l1 = lax.ppermute(t1, "tp", move_y(1)), lax.ppermute(t1, "tp", move_y(-1))
    o0, o1 = lax.ppermute(r0, "tp", move_y(1)), lax.ppermute(l1, "tp", move_y(-1))
    tiles = []
    for mine in (t0, t1, l0, l1, o0, o1, r0, r1):
        tiles += [mine, lax.ppermute(mine, "tp", SWAP_CORE)]

    parts = run_fwd(me, mods[0], ref_h, ref_w)
    summed = [add(parts[2 * r], lax.ppermute(parts[2 * r + 1], "tp", SWAP_CORE)) for r in range(NY)]
    from_l = lax.ppermute(summed[2][0], "tp", move_y(1))
    from_r = lax.ppermute(summed[2][1], "tp", move_y(-1))
    up0 = lax.ppermute(add(summed[1][0], from_l), "tp", move_y(1))
    up1 = lax.ppermute(summed[1][1], "tp", move_y(1))
    dn0 = lax.ppermute(summed[3][0], "tp", move_y(-1))
    dn1 = lax.ppermute(add(summed[3][1], from_r), "tp", move_y(-1))
    mine = add(summed[0][0], up0, dn0)
    other = add(summed[0][1], up1, dn1)
    mine = add(mine, lax.ppermute(other, "tp", SWAP_ZHI))
    mine = lax.ppermute(mine, ("fsdp", "tp"), FROM_GROUP)
    ref_out = (mine.T.astype(F32) + ref_residual.astype(F32)).astype(BF16)

    dh = run_dh(me, mods[1], tiles, pol_w)
    own_a, own_b, p1a, p1b, p2a, p2b, p3a, p3b = dh
    in_a = lax.ppermute(p2a, "fsdp", move_x(1))
    in_b = lax.ppermute(p2b, "fsdp", move_x(-1))
    r_b = lax.ppermute(p1b, "fsdp", move_x(1))
    l_a = lax.ppermute(p3a, "fsdp", move_x(-1))
    r_a = lax.ppermute(add(p1a, in_a), "fsdp", move_x(1))
    l_b = lax.ppermute(add(p3b, in_b), "fsdp", move_x(-1))
    d_a = own_a + r_a.astype(F32) + l_a.astype(F32)
    d_b = own_b + r_b.astype(F32) + l_b.astype(F32)
    d_hidden = jnp.concatenate([d_a, d_b], axis=1)
    gate_late, up_late, _ = lax.optimization_barrier((pol_gate_t, pol_up_t, own_a))
    gate_f, up_f = gate_late.astype(F32), up_late.astype(F32)
    sig = jax.nn.sigmoid(gate_f)
    grad_gate = (d_hidden * up_f * sig * (1.0 + gate_f * (1.0 - sig))).astype(BF16).T
    grad_up = (d_hidden * (gate_f * sig)).astype(BF16).T

    own_t, own_i, send_t, send_i = run_dw(me, mods[1], tiles, pol_h)
    grad_text = (own_t + lax.ppermute(send_t, "fsdp", SWAP_ZLO).astype(F32)).T
    grad_image = (own_i + lax.ppermute(send_i, "fsdp", SWAP_ZLO).astype(F32)).T
    return (ref_out, grad_gate, grad_up, grad_text, grad_image)


def solution(mesh):
    both = P("fsdp", "tp")
    rows = P("fsdp")
    in_specs = (
        both,
        both,
        both,
        rows,
        both,
        both,
        both,
        both,
        rows,
        rows,
        P(),
        both,
        both,
        both,
    )
    return jax.shard_map(
        per_device, mesh=mesh, in_specs=in_specs, out_specs=(both,) * 5, check_vma=False
    )
```

time: 529 us -> 269 us (0.51)
  the two profiles are of different devices: /device:TPU:0 before, /device:TPU:6 now
where the time goes in v1:
time: 269 us; the launch traced here: 268 us
  waiting for transfers between devices  124 us (46%)
  starting transfers between devices  63.5 us (24%)
  Pallas kernels  54.2 us (20%)
  other arithmetic  19.4 us (7%)
  local copies, waits for them, and re-layouts  5.52 us (2%)
    pallas_call x1, Pallas kernels, run_dh(): pl.pallas_call(dh_kernel, name='dh', out_shape=[jax.ShapeDtypeStruct((uni...  20.1 us
    pallas_call x1, Pallas kernels, run_fwd(): pl.pallas_call(fwd_kernel, name='fwd', out_shape=[jax.ShapeDtypeStruct((2...  17.9 us
    pallas_call x1, Pallas kernels, run_dw(): pl.pallas_call(dw_kernel, name='dw', out_shape=[jax.ShapeDtypeStruct((uni...  16.3 us
    ppermute x1, waiting for transfers between devices, per_device(): in_b = lax.ppermute(p2b, 'fsdp', move_x(-1))  14.4 us
    ppermute x4, waiting for transfers between devices, both_rows(): return own + tuple((lax.ppermute(w, 'fsdp', SWAP_ZLO) for w in own))  14.3 us
    ppermute x1, waiting for transfers between devices, per_device(): mine = lax.ppermute(mine, ('fsdp', 'tp'), FROM_GROUP)  12.9 us
    ppermute x1, waiting for transfers between devices, per_device(): mod_o = lax.ppermute(mod_r, 'fsdp', move_x(1))  10.8 us
    ppermute x2, waiting for transfers between devices, gather_x(): opp_b = lax.ppermute(left[split:], 'fsdp', move_x(-1))  10.2 us
  transfers between devices with their start and end apart: 51, of which 20 were waited for; matrix products, arithmetic and copies ran while one was open for 8% of the time, Pallas kernels for 20%

profile of v1, /device:TPU:6, one launch (start us, length us, event | category | flops | bytes accessed | tf_op | source)
XLA Modules:
  0.0 268.1 jit_solution(12452222671995829043)
XLA Ops:
  2.5 1.7 collective-permute-start
  4.1 1.9 collective-permute-start.7
  7.6 1.2 multiply_convert_fusion
  8.8 6.0 %collective-permute-start.21 = (bf16[768,256]{1,0:T(8,128)(2,1)S(1)}, bf16[768,256]{1,0:T(8,128)(2,1)S(1)}, u32[]{:S(2)}, u32[]{:S(2)}) collective-permute-start(bf16[768,256]{1,0:T(8,128)(2,1)S(1)} %multiply_convert_fusion), channel_id=1, source_target_pairs={{0,0},{1,1},{2,28},{3,29},{4,40},{5,41},{6,52},{7,53},{8,2},{9,3},... | collective-permute-start | bytes 1179656 | tf_op jit(solution)/shard_map/ppermute | solution.py:329
  14.9 2.9 %collective-permute-start.8 = (bf16[688,512]{1,0:T(8,128)(2,1)}, bf16[688,512]{1,0:T(8,128)(2,1)S(1)}, u32[]{:S(2)}, u32[]{:S(2)}) collective-permute-start(bf16[688,512]{1,0:T(8,128)(2,1)} %bitcast.82), channel_id=1, source_target_pairs={{0,64},{16,80},{32,96},{48,112},{64,0},{80,16},{96,32},{112,48},{1... | collective-permute-start | bytes 2113544 | tf_op jit(solution)/shard_map/ppermute | solution.py:343
  17.8 2.2 fusion.16.refs_16_
  20.7 10.8 %collective-permute-done.2 = s32[2,768]{1,0:T(2,128)S(1)} collective-permute-done((s32[2,768]{1,0:T(2,128)S(1)}, s32[2,768]{1,0:T(2,128)S(1)}, u32[]{:S(2)}, u32[]{:S(2)}) %collective-permute-start.2) | collective-permute-done | bytes 6176 | tf_op jit(solution)/shard_map/ppermute | solution.py:334
  32.2 5.6 %collective-permute-start.29 = (bf16[768,256]{1,0:T(8,128)(2,1)S(1)}, bf16[768,256]{1,0:T(8,128)(2,1)S(1)}, u32[]{:S(2)}, u32[]{:S(2)}) collective-permute-start(bf16[768,256]{1,0:T(8,128)(2,1)S(1)} %collective-permute-done.21.refs_0_), channel_id=1, source_target_pairs={{0,4},{1,5},{2,6},{3,7},{4,8},{5,9},{6,10},{7,11},{8,12},{9,13},{1... | collective-permute-start | bytes 1179656 | tf_op jit(solution)/shard_map/ppermute | solution.py:349
  38.6 9.5 %collective-permute-start.4 = (bf16[688,768]{1,0:T(8,128)(2,1)S(1)}, bf16[688,768]{1,0:T(8,128)(2,1)S(1)}, u32[]{:S(2)}, u32[]{:S(2)}) collective-permute-start(bf16[688,768]{1,0:T(8,128)(2,1)S(1)} %fusion.12.refs_0_), channel_id=1, source_target_pairs={{0,16},{16,32},{32,48},{48,0},{64,80},{80,96},{96,112},{112,64},{1... | collective-permute-start | bytes 3170312 | tf_op jit(solution)/shard_map/ppermute | solution.py:291
  48.1 8.6 %collective-permute-done.23.refs_2_ = bf16[768,256]{1,0:T(8,128)(2,1)S(1)} collective-permute-done((bf16[768,256]{1,0:T(8,128)(2,1)S(1)}, bf16[768,256]{1,0:T(8,128)(2,1)S(1)}, u32[]{:S(2)}, u32[]{:S(2)}) %collective-permute-start.23) | collective-permute-done | bytes 393248 | tf_op jit(solution)/shard_map/ppermute | solution.py:348
  56.7 3.1 %collective-permute-start.25 = (bf16[768,256]{1,0:T(8,128)(2,1)S(1)}, bf16[768,256]{1,0:T(8,128)(2,1)S(1)}, u32[]{:S(2)}, u32[]{:S(2)}) collective-permute-start(bf16[768,256]{1,0:T(8,128)(2,1)S(1)} %collective-permute-done.21.refs_0_), channel_id=1, source_target_pairs={{0,12},{1,13},{2,14},{3,15},{4,0},{5,1},{6,2},{7,3},{8,4},{9,5},{1... | collective-permute-start | bytes 1179656 | tf_op jit(solution)/shard_map/ppermute | solution.py:349
  59.8 7.0 %collective-permute-done.25.refs_4_ = bf16[768,256]{1,0:T(8,128)(2,1)S(1)} collective-permute-done((bf16[768,256]{1,0:T(8,128)(2,1)S(1)}, bf16[768,256]{1,0:T(8,128)(2,1)S(1)}, u32[]{:S(2)}, u32[]{:S(2)}) %collective-permute-start.25) | collective-permute-done | bytes 393248 | tf_op jit(solution)/shard_map/ppermute | solution.py:349
  66.8 1.7 collective-permute-done.22.refs_1_
  68.5 3.7 %collective-permute-start.27 = (bf16[768,256]{1,0:T(8,128)(2,1)S(1)}, bf16[768,256]{1,0:T(8,128)(2,1)S(1)}, u32[]{:S(2)}, u32[]{:S(2)}) collective-permute-start(bf16[768,256]{1,0:T(8,128)(2,1)S(1)} %collective-permute-done.23.refs_2_), channel_id=1, source_target_pairs={{0,12},{1,13},{2,14},{3,15},{4,0},{5,1},{6,2},{7,3},{8,4},{9,5},{1... | collective-permute-start | bytes 1179656 | tf_op jit(solution)/shard_map/ppermute | solution.py:350
  72.3 3.9 %collective-permute-done.4.refs_4_ = bf16[688,768]{1,0:T(8,128)(2,1)S(1)} collective-permute-done((bf16[688,768]{1,0:T(8,128)(2,1)S(1)}, bf16[688,768]{1,0:T(8,128)(2,1)S(1)}, u32[]{:S(2)}, u32[]{:S(2)}) %collective-permute-start.4) | collective-permute-done | bytes 1056800 | tf_op jit(solution)/shard_map/ppermute | solution.py:291
  76.2 5.3 %collective-permute-done.3.refs_1_ = bf16[688,768]{1,0:T(8,128)(2,1)S(1)} collective-permute-done((bf16[688,768]{1,0:T(8,128)(2,1)S(1)}, bf16[688,768]{1,0:T(8,128)(2,1)S(1)}, u32[]{:S(2)}, u32[]{:S(2)}) %collective-permute-start.3) | collective-permute-done | bytes 1056800 | tf_op jit(solution)/shard_map/ppermute | solution.py:292
  81.7 2.1 collective-permute-start.5
  83.9 1.5 collective-permute-done.35.refs_14_
  86.4 6.3 %collective-permute-done.30.refs_8_ = bf16[768,256]{1,0:T(8,128)(2,1)S(1)} collective-permute-done((bf16[768,256]{1,0:T(8,128)(2,1)S(1)}, bf16[768,256]{1,0:T(8,128)(2,1)S(1)}, u32[]{:S(2)}, u32[]{:S(2)}) %collective-permute-start.30) | collective-permute-done | bytes 393248 | tf_op jit(solution)/shard_map/ppermute | solution.py:351
  96.6 2.5 collective-permute-start.47
  99.1 1.7 collective-permute-done.48.refs_19_
  100.8 8.5 %collective-permute-done.6.refs_3_ = bf16[336,768]{1,0:T(8,128)(2,1)} collective-permute-done((bf16[336,768]{1,0:T(8,128)(2,1)S(1)}, bf16[336,768]{1,0:T(8,128)(2,1)}, u32[]{:S(2)}, u32[]{:S(2)}) %collective-permute-start.6) | collective-permute-done | bytes 516128 | tf_op jit(solution)/shard_map/ppermute | solution.py:294
  110.7 17.9 %fwd.1 = (bf16[2,256,768]{2,1,0:T(8,128)(2,1)}, bf16[2,256,768]{2,1,0:T(8,128)(2,1)}, bf16[2,256,768]{2,1,0:T(8,128)(2,1)}, bf16[2,256,768]{2,1,0:T(8,128)(2,1)}...) custom-call(s32[3]{0:T(128)} %pad_add_fusion.2.me_ref, ...), custom_call_target="tpu_custom_call" | custom-call | flops 8657043456 | bytes 14000000 | tf_op jit(solution)/shard_map/fwd/pallas_call | solution.py:264
  128.6 1.9 collective-permute-start.37
  131.3 16.3 %dw.1 = (f32[688,512]{1,0:T(8,128)}, f32[688,512]{1,0:T(8,128)}, bf16[688,512]{1,0:T(8,128)(2,1)}, bf16[688,512]{1,0:T(8,128)(2,1)}) custom-call(s32[3]{0:T(128)} %pad_add_fusion.2.me_ref, s32[4,768]{1,0:T(4,128)} %get-tuple-element.68.mod_ref, bf16[768,256]{1,0:T(8,128)(2,1)} %copy-done.27, bf16[768,256]{1,0:T(8,128)(2,1)} %copy-done.31, ...), custom_call_target="tpu_custom_call" | custom-call | flops 8657043456 | bytes 20000000 | tf_op jit(solution)/shard_map/dw/pallas_call | solution.py:120
  148.1 14.3 %collective-permute-done.38.refs_19_ = bf16[688,512]{1,0:T(8,128)(2,1)} collective-permute-done((bf16[688,512]{1,0:T(8,128)(2,1)}, bf16[688,512]{1,0:T(8,128)(2,1)}, u32[]{:S(2)}, u32[]{:S(2)}) %collective-permute-start.38) | collective-permute-done | bytes 704544 | tf_op jit(solution)/shard_map/ppermute | solution.py:343
  162.4 1.7 collective-permute-start.50
  164.1 20.1 %dh.1 = (f32[688,384]{1,0:T(8,128)}, f32[688,384]{1,0:T(8,128)}, bf16[688,384]{1,0:T(8,128)(2,1)}, bf16[688,384]{1,0:T(8,128)(2,1)}, bf16[688,384]{1,0:T(8,128)(...) custom-call(s32[3]{0:T(128)} %pad_add_fusion.2.me_ref, ...), custom_call_target="tpu_custom_call" | custom-call | flops 8657043456 | bytes 16000000 | tf_op jit(solution)/shard_map/dh/pallas_call | solution.py:192
  184.6 1.6 add_convert_fusion.2
  186.1 1.6 collective-permute-start.39
  187.8 1.3 add_convert_fusion.1
  189.7 1.3 add_convert_fusion.3
  191.2 1.3 add_convert_fusion
  192.7 6.7 %collective-permute-done.39 = bf16[688,384]{1,0:T(8,128)(2,1)S(1)} collective-permute-done((bf16[688,384]{1,0:T(8,128)(2,1)S(1)}, bf16[688,384]{1,0:T(8,128)(2,1)S(1)}, u32[]{:S(2)}, u32[]{:S(2)}) %collective-permute-start.39) | collective-permute-done | bytes 528416 | tf_op jit(solution)/shard_map/ppermute | solution.py:372
  200.0 14.4 %collective-permute-done.43 = bf16[688,384]{1,0:T(8,128)(2,1)S(1)} collective-permute-done((bf16[688,384]{1,0:T(8,128)(2,1)S(1)}, bf16[688,384]{1,0:T(8,128)(2,1)S(1)}, u32[]{:S(2)}, u32[]{:S(2)}) %collective-permute-start.43) | collective-permute-done | bytes 528416 | tf_op jit(solution)/shard_map/ppermute | solution.py:373
  214.4 2.1 collective-permute-start.17
  216.8 2.5 add_bitcast_fusion
  219.4 4.1 %collective-permute-done.17 = bf16[256,768]{1,0:T(8,128)(2,1)S(1)} collective-permute-done((bf16[256,768]{1,0:T(8,128)(2,1)S(1)}, bf16[256,768]{1,0:T(8,128)(2,1)S(1)}, u32[]{:S(2)}, u32[]{:S(2)}) %collective-permute-start.17) | collective-permute-done | bytes 393248 | tf_op jit(solution)/shard_map/ppermute | solution.py:359
  223.5 3.7 %collective-permute-start.18 = (bf16[256,768]{1,0:T(8,128)(2,1)S(1)}, bf16[256,768]{1,0:T(8,128)(2,1)S(1)}, u32[]{:S(2)}, u32[]{:S(2)}) collective-permute-start(bf16[256,768]{1,0:T(8,128)(2,1)S(1)} %fusion.19), channel_id=1, source_target_pairs={{0,12},{1,13},{2,14},{3,15},{4,0},{5,1},{6,2},{7,3},{8,4},{9,5},{1... | collective-permute-start | bytes 1179656 | tf_op jit(solution)/shard_map/ppermute | solution.py:363
  227.2 1.3 add_bitcast_fusion.1
  228.5 1.4 collective-permute-start.42
  230.1 6.6 %collective-permute-done.18 = bf16[256,768]{1,0:T(8,128)(2,1)S(1)} collective-permute-done((bf16[256,768]{1,0:T(8,128)(2,1)S(1)}, bf16[256,768]{1,0:T(8,128)(2,1)S(1)}, u32[]{:S(2)}, u32[]{:S(2)}) %collective-permute-start.18) | collective-permute-done | bytes 393248 | tf_op jit(solution)/shard_map/ppermute | solution.py:363
  236.7 2.0 collective-permute-start.44
  239.3 6.6 %collective-permute-done.42 = bf16[688,384]{1,0:T(8,128)(2,1)S(1)} collective-permute-done((bf16[688,384]{1,0:T(8,128)(2,1)S(1)}, bf16[688,384]{1,0:T(8,128)(2,1)S(1)}, u32[]{:S(2)}, u32[]{:S(2)}) %collective-permute-start.42) | collective-permute-done | bytes 528416 | tf_op jit(solution)/shard_map/ppermute | solution.py:374
  245.9 1.2 collective-permute-done.44
  248.6 3.1 %collective-permute-start.20 = (bf16[256,768]{1,0:T(8,128)(2,1)S(1)}, bf16[256,768]{1,0:T(8,128)(2,1)S(1)}, u32[]{:S(2)}, u32[]{:S(2)}) collective-permute-start(bf16[256,768]{1,0:T(8,128)(2,1)S(1)} %add_convert_fusion.6), channel_id=1, source_target_pairs={{0,0},{1,1},{28,2},{29,3},{40,4},{41,5},{52,6},{53,7},{2,8},{3,9},... | collective-permute-start | bytes 1179656 | tf_op jit(solution)/shard_map/ppermute | solution.py:367
  251.7 2.4 fusion.17
  254.2 12.9 %collective-permute-done.20 = bf16[256,768]{1,0:T(8,128)(2,1)S(1)} collective-permute-done((bf16[256,768]{1,0:T(8,128)(2,1)S(1)}, bf16[256,768]{1,0:T(8,128)(2,1)S(1)}, u32[]{:S(2)}, u32[]{:S(2)}) %collective-permute-start.20) | collective-permute-done | bytes 393248 | tf_op jit(solution)/shard_map/ppermute | solution.py:367
  (170 shorter events, 18.5 us)
Async XLA Ops:
  2.0 15.8 %collective-permute-start.1 = (s32[2,768]{1,0:T(2,128)S(1)}, s32[2,768]{1,0:T(2,128)S(1)}, u32[]{:S(2)}, u32[]{:S(2)}) collective-permute-start(s32[2,768]{1,0:T(2,128)S(1)} %get-tuple-element.71), channel_id=1, source_target_pairs={{0,16},{16,32},{32,48},{48,0},{64,80},{80,96},{96,112},{112,64},{1... | collective-permute-start | bytes 18440 | tf_op jit(solution)/shard_map/ppermute | solution.py:332
  2.5 17.5 %collective-permute-start = (s32[2,768]{1,0:T(2,128)S(1)}, s32[2,768]{1,0:T(2,128)S(1)}, u32[]{:S(2)}, u32[]{:S(2)}) collective-permute-start(s32[2,768]{1,0:T(2,128)S(1)} %get-tuple-element.71), channel_id=1, source_target_pairs={{0,48},{16,0},{32,16},{48,32},{64,112},{80,64},{96,80},{112,96},{1... | collective-permute-start | bytes 18440 | tf_op jit(solution)/shard_map/ppermute | solution.py:333
  4.1 28.0 %collective-permute-start.7 = (bf16[688,512]{1,0:T(8,128)(2,1)}, bf16[688,512]{1,0:T(8,128)(2,1)S(1)}, u32[]{:S(2)}, u32[]{:S(2)}) collective-permute-start(bf16[688,512]{1,0:T(8,128)(2,1)} %bitcast.80), channel_id=1, source_target_pairs={{0,64},{16,80},{32,96},{48,112},{64,0},{80,16},{96,32},{112,48},{1... | collective-permute-start | bytes 2113544 | tf_op jit(solution)/shard_map/ppermute | solution.py:343
  8.8 23.3 %collective-permute-start.21 = (bf16[768,256]{1,0:T(8,128)(2,1)S(1)}, bf16[768,256]{1,0:T(8,128)(2,1)S(1)}, u32[]{:S(2)}, u32[]{:S(2)}) collective-permute-start(bf16[768,256]{1,0:T(8,128)(2,1)S(1)} %multiply_convert_fusion), channel_id=1, source_target_pairs={{0,0},{1,1},{2,28},{3,29},{4,40},{5,41},{6,52},{7,53},{8,2},{9,3},... | collective-permute-start | bytes 1179656 | tf_op jit(solution)/shard_map/ppermute | solution.py:329
  14.9 23.7 %collective-permute-start.8 = (bf16[688,512]{1,0:T(8,128)(2,1)}, bf16[688,512]{1,0:T(8,128)(2,1)S(1)}, u32[]{:S(2)}, u32[]{:S(2)}) collective-permute-start(bf16[688,512]{1,0:T(8,128)(2,1)} %bitcast.82), channel_id=1, source_target_pairs={{0,64},{16,80},{32,96},{48,112},{64,0},{80,16},{96,32},{112,48},{1... | collective-permute-start | bytes 2113544 | tf_op jit(solution)/shard_map/ppermute | solution.py:343
  17.8 13.7 %collective-permute-start.2 = (s32[2,768]{1,0:T(2,128)S(1)}, s32[2,768]{1,0:T(2,128)S(1)}, u32[]{:S(2)}, u32[]{:S(2)}) collective-permute-start(s32[2,768]{1,0:T(2,128)S(1)} %collective-permute-done.1), channel_id=1, source_target_pairs={{0,16},{16,32},{32,48},{48,0},{64,80},{80,96},{96,112},{112,64},{1... | collective-permute-start | bytes 18440 | tf_op jit(solution)/shard_map/ppermute | solution.py:334
  20.0 52.2 %collective-permute-start.46 = (bf16[688,768]{1,0:T(8,128)(2,1)S(1)}, bf16[688,768]{1,0:T(8,128)(2,1)S(1)}, u32[]{:S(2)}, u32[]{:S(2)}) collective-permute-start(bf16[688,768]{1,0:T(8,128)(2,1)S(1)} %fusion.16.refs_16_), channel_id=1, source_target_pairs={{0,16},{16,32},{32,48},{48,0},{64,80},{80,96},{96,112},{112,64},{1... | collective-permute-start | bytes 3170312 | tf_op jit(solution)/shard_map/ppermute | solution.py:291
  31.5 40.7 %collective-permute-start.45 = (bf16[688,768]{1,0:T(8,128)(2,1)S(1)}, bf16[688,768]{1,0:T(8,128)(2,1)S(1)}, u32[]{:S(2)}, u32[]{:S(2)}) collective-permute-start(bf16[688,768]{1,0:T(8,128)(2,1)S(1)} %fusion.16.refs_16_), channel_id=1, source_target_pairs={{0,48},{16,0},{32,16},{48,32},{64,112},{80,64},{96,80},{112,96},{1... | collective-permute-start | bytes 3170312 | tf_op jit(solution)/shard_map/ppermute | solution.py:292
  32.2 24.6 %collective-permute-start.23 = (bf16[768,256]{1,0:T(8,128)(2,1)S(1)}, bf16[768,256]{1,0:T(8,128)(2,1)S(1)}, u32[]{:S(2)}, u32[]{:S(2)}) collective-permute-start(bf16[768,256]{1,0:T(8,128)(2,1)S(1)} %collective-permute-done.21.refs_0_), channel_id=1, source_target_pairs={{0,2},{1,3},{2,0},{3,1},{4,6},{5,7},{6,4},{7,5},{8,10},{9,11},{10,... | collective-permute-start | bytes 1179656 | tf_op jit(solution)/shard_map/ppermute | solution.py:348
  32.2 24.5 %collective-permute-start.29 = (bf16[768,256]{1,0:T(8,128)(2,1)S(1)}, bf16[768,256]{1,0:T(8,128)(2,1)S(1)}, u32[]{:S(2)}, u32[]{:S(2)}) collective-permute-start(bf16[768,256]{1,0:T(8,128)(2,1)S(1)} %collective-permute-done.21.refs_0_), channel_id=1, source_target_pairs={{0,4},{1,5},{2,6},{3,7},{4,8},{5,9},{6,10},{7,11},{8,12},{9,13},{1... | collective-permute-start | bytes 1179656 | tf_op jit(solution)/shard_map/ppermute | solution.py:349
  38.6 37.6 %collective-permute-start.4 = (bf16[688,768]{1,0:T(8,128)(2,1)S(1)}, bf16[688,768]{1,0:T(8,128)(2,1)S(1)}, u32[]{:S(2)}, u32[]{:S(2)}) collective-permute-start(bf16[688,768]{1,0:T(8,128)(2,1)S(1)} %fusion.12.refs_0_), channel_id=1, source_target_pairs={{0,16},{16,32},{32,48},{48,0},{64,80},{80,96},{96,112},{112,64},{1... | collective-permute-start | bytes 3170312 | tf_op jit(solution)/shard_map/ppermute | solution.py:291
  56.7 24.9 %collective-permute-start.3 = (bf16[688,768]{1,0:T(8,128)(2,1)S(1)}, bf16[688,768]{1,0:T(8,128)(2,1)S(1)}, u32[]{:S(2)}, u32[]{:S(2)}) collective-permute-start(bf16[688,768]{1,0:T(8,128)(2,1)S(1)} %fusion.12.refs_0_), channel_id=1, source_target_pairs={{0,48},{16,0},{32,16},{48,32},{64,112},{80,64},{96,80},{112,96},{1... | collective-permute-start | bytes 3170312 | tf_op jit(solution)/shard_map/ppermute | solution.py:292
  56.7 10.0 %collective-permute-start.25 = (bf16[768,256]{1,0:T(8,128)(2,1)S(1)}, bf16[768,256]{1,0:T(8,128)(2,1)S(1)}, u32[]{:S(2)}, u32[]{:S(2)}) collective-permute-start(bf16[768,256]{1,0:T(8,128)(2,1)S(1)} %collective-permute-done.21.refs_0_), channel_id=1, source_target_pairs={{0,12},{1,13},{2,14},{3,15},{4,0},{5,1},{6,2},{7,3},{8,4},{9,5},{1... | collective-permute-start | bytes 1179656 | tf_op jit(solution)/shard_map/ppermute | solution.py:349
  68.5 13.1 %collective-permute-start.27 = (bf16[768,256]{1,0:T(8,128)(2,1)S(1)}, bf16[768,256]{1,0:T(8,128)(2,1)S(1)}, u32[]{:S(2)}, u32[]{:S(2)}) collective-permute-start(bf16[768,256]{1,0:T(8,128)(2,1)S(1)} %collective-permute-done.23.refs_2_), channel_id=1, source_target_pairs={{0,12},{1,13},{2,14},{3,15},{4,0},{5,1},{6,2},{7,3},{8,4},{9,5},{1... | collective-permute-start | bytes 1179656 | tf_op jit(solution)/shard_map/ppermute | solution.py:350
  72.2 13.2 %collective-permute-start.35 = (bf16[768,256]{1,0:T(8,128)(2,1)S(1)}, bf16[768,256]{1,0:T(8,128)(2,1)S(1)}, u32[]{:S(2)}, u32[]{:S(2)}) collective-permute-start(bf16[768,256]{1,0:T(8,128)(2,1)S(1)} %collective-permute-done.23.refs_2_), channel_id=1, source_target_pairs={{0,4},{1,5},{2,6},{3,7},{4,8},{5,9},{6,10},{7,11},{8,12},{9,13},{1... | collective-permute-start | bytes 1179656 | tf_op jit(solution)/shard_map/ppermute | solution.py:350
  72.2 20.5 %collective-permute-start.30 = (bf16[768,256]{1,0:T(8,128)(2,1)S(1)}, bf16[768,256]{1,0:T(8,128)(2,1)S(1)}, u32[]{:S(2)}, u32[]{:S(2)}) collective-permute-start(bf16[768,256]{1,0:T(8,128)(2,1)S(1)} %collective-permute-done.29.refs_12_), channel_id=1, source_target_pairs={{0,4},{1,5},{2,6},{3,7},{4,8},{5,9},{6,10},{7,11},{8,12},{9,13},{1... | collective-permute-start | bytes 1179656 | tf_op jit(solution)/shard_map/ppermute | solution.py:351
  76.2 17.6 %collective-permute-start.24 = (bf16[768,256]{1,0:T(8,128)(2,1)S(1)}, bf16[768,256]{1,0:T(8,128)(2,1)}, u32[]{:S(2)}, u32[]{:S(2)}) collective-permute-start(bf16[768,256]{1,0:T(8,128)(2,1)S(1)} %collective-permute-done.23.refs_2_), channel_id=1, source_target_pairs={{0,1},{1,0},{2,3},{3,2},{4,5},{5,4},{6,7},{7,6},{8,9},{9,8},{10,11... | collective-permute-start | bytes 1179656 | tf_op jit(solution)/shard_map/ppermute | solution.py:354
  81.6 12.3 %collective-permute-start.34 = (bf16[768,256]{1,0:T(8,128)(2,1)S(1)}, bf16[768,256]{1,0:T(8,128)(2,1)}, u32[]{:S(2)}, u32[]{:S(2)}) collective-permute-start(bf16[768,256]{1,0:T(8,128)(2,1)S(1)} %collective-permute-done.29.refs_12_), channel_id=1, source_target_pairs={{0,1},{1,0},{2,3},{3,2},{4,5},{5,4},{6,7},{7,6},{8,9},{9,8},{10,11... | collective-permute-start | bytes 1179656 | tf_op jit(solution)/shard_map/ppermute | solution.py:354
  81.7 28.2 %collective-permute-start.5 = (bf16[352,768]{1,0:T(8,128)(2,1)S(1)}, bf16[352,768]{1,0:T(8,128)(2,1)S(1)}, u32[]{:S(2)}, u32[]{:S(2)}) collective-permute-start(bf16[352,768]{1,0:T(8,128)(2,1)S(1)} %slice.58), channel_id=1, source_target_pairs={{0,16},{16,32},{32,48},{48,0},{64,80},{80,96},{96,112},{112,64},{1... | collective-permute-start | bytes 1622024 | tf_op jit(solution)/shard_map/ppermute | solution.py:293
  85.4 15.4 %collective-permute-start.48 = (bf16[336,768]{1,0:T(8,128)(2,1)S(1)}, bf16[336,768]{1,0:T(8,128)(2,1)}, u32[]{:S(2)}, u32[]{:S(2)}) collective-permute-start(bf16[336,768]{1,0:T(8,128)(2,1)S(1)} %slice.70), channel_id=1, source_target_pairs={{0,48},{16,0},{32,16},{48,32},{64,112},{80,64},{96,80},{112,96},{1... | collective-permute-start | bytes 1548296 | tf_op jit(solution)/shard_map/ppermute | solution.py:294
  92.7 16.6 %collective-permute-start.6 = (bf16[336,768]{1,0:T(8,128)(2,1)S(1)}, bf16[336,768]{1,0:T(8,128)(2,1)}, u32[]{:S(2)}, u32[]{:S(2)}) collective-permute-start(bf16[336,768]{1,0:T(8,128)(2,1)S(1)} %slice.59), channel_id=1, source_target_pairs={{0,48},{16,0},{32,16},{48,32},{64,112},{80,64},{96,80},{112,96},{1... | collective-permute-start | bytes 1548296 | tf_op jit(solution)/shard_map/ppermute | solution.py:294
  93.9 15.4 %collective-permute-start.32 = (bf16[768,256]{1,0:T(8,128)(2,1)}, bf16[768,256]{1,0:T(8,128)(2,1)}, u32[]{:S(2)}, u32[]{:S(2)}) collective-permute-start(bf16[768,256]{1,0:T(8,128)(2,1)} %copy-done.32), channel_id=1, source_target_pairs={{0,12},{1,13},{2,14},{3,15},{4,0},{5,1},{6,2},{7,3},{8,4},{9,5},{1... | collective-permute-start | bytes 1179656 | tf_op jit(solution)/shard_map/ppermute | solution.py:351
  96.6 34.2 %collective-permute-start.47 = (bf16[352,768]{1,0:T(8,128)(2,1)S(1)}, bf16[352,768]{1,0:T(8,128)(2,1)}, u32[]{:S(2)}, u32[]{:S(2)}) collective-permute-start(bf16[352,768]{1,0:T(8,128)(2,1)S(1)} %slice.69), channel_id=1, source_target_pairs={{0,16},{16,32},{32,48},{48,0},{64,80},{80,96},{96,112},{112,64},{1... | collective-permute-start | bytes 1622024 | tf_op jit(solution)/shard_map/ppermute | solution.py:293
  100.8 27.8 %collective-permute-start.28 = (bf16[768,256]{1,0:T(8,128)(2,1)}, bf16[768,256]{1,0:T(8,128)(2,1)}, u32[]{:S(2)}, u32[]{:S(2)}) collective-permute-start(bf16[768,256]{1,0:T(8,128)(2,1)} %copy-done.32), channel_id=1, source_target_pairs={{0,1},{1,0},{2,3},{3,2},{4,5},{5,4},{6,7},{7,6},{8,9},{9,8},{10,11... | collective-permute-start | bytes 1179656 | tf_op jit(solution)/shard_map/ppermute | solution.py:354
  109.3 21.2 %collective-permute-start.36 = (bf16[768,256]{1,0:T(8,128)(2,1)}, bf16[768,256]{1,0:T(8,128)(2,1)}, u32[]{:S(2)}, u32[]{:S(2)}) collective-permute-start(bf16[768,256]{1,0:T(8,128)(2,1)} %copy-done.33), channel_id=1, source_target_pairs={{0,1},{1,0},{2,3},{3,2},{4,5},{5,4},{6,7},{7,6},{8,9},{9,8},{10,11... | collective-permute-start | bytes 1179656 | tf_op jit(solution)/shard_map/ppermute | solution.py:354
  109.3 21.3 %collective-permute-start.31 = (bf16[768,256]{1,0:T(8,128)(2,1)}, bf16[768,256]{1,0:T(8,128)(2,1)}, u32[]{:S(2)}, u32[]{:S(2)}) collective-permute-start(bf16[768,256]{1,0:T(8,128)(2,1)} %copy-done.34), channel_id=1, source_target_pairs={{0,1},{1,0},{2,3},{3,2},{4,5},{5,4},{6,7},{7,6},{8,9},{9,8},{10,11... | collective-permute-start | bytes 1179656 | tf_op jit(solution)/shard_map/ppermute | solution.py:354
  110.6 20.5 %collective-permute-start.33 = (bf16[768,256]{1,0:T(8,128)(2,1)}, bf16[768,256]{1,0:T(8,128)(2,1)}, u32[]{:S(2)}, u32[]{:S(2)}) collective-permute-start(bf16[768,256]{1,0:T(8,128)(2,1)} %collective-permute-done.32.refs_10_), channel_id=1, source_target_pairs={{0,1},{1,0},{2,3},{3,2},{4,5},{5,4},{6,7},{7,6},{8,9},{9,8},{10,11... | collective-permute-start | bytes 1179656 | tf_op jit(solution)/shard_map/ppermute | solution.py:354
  128.6 19.1 %collective-permute-start.37 = (bf16[688,512]{1,0:T(8,128)(2,1)}, bf16[688,512]{1,0:T(8,128)(2,1)}, u32[]{:S(2)}, u32[]{:S(2)}) collective-permute-start(bf16[688,512]{1,0:T(8,128)(2,1)} %bitcast.84), channel_id=1, source_target_pairs={{0,64},{16,80},{32,96},{48,112},{64,0},{80,16},{96,32},{112,48},{1... | collective-permute-start | bytes 2113544 | tf_op jit(solution)/shard_map/ppermute | solution.py:343
  130.5 31.9 %collective-permute-start.38 = (bf16[688,512]{1,0:T(8,128)(2,1)}, bf16[688,512]{1,0:T(8,128)(2,1)}, u32[]{:S(2)}, u32[]{:S(2)}) collective-permute-start(bf16[688,512]{1,0:T(8,128)(2,1)} %bitcast.86), channel_id=1, source_target_pairs={{0,64},{16,80},{32,96},{48,112},{64,0},{80,16},{96,32},{112,48},{1... | collective-permute-start | bytes 2113544 | tf_op jit(solution)/shard_map/ppermute | solution.py:343
  130.7 53.5 %collective-permute-start.10 = (bf16[2,256,768]{2,1,0:T(8,128)(2,1)}, bf16[2,256,768]{2,1,0:T(8,128)(2,1)}, u32[]{:S(2)}, u32[]{:S(2)}) collective-permute-start(bf16[2,256,768]{2,1,0:T(8,128)(2,1)} %get-tuple-element.30), channel_id=1, source_target_pairs={{0,1},{1,0},{2,3},{3,2},{4,5},{5,4},{6,7},{7,6},{8,9},{9,8},{10,11... | collective-permute-start | bytes 2359304 | tf_op jit(solution)/shard_map/ppermute | solution.py:357
  130.8 55.3 %collective-permute-start.11 = (bf16[2,256,768]{2,1,0:T(8,128)(2,1)}, bf16[2,256,768]{2,1,0:T(8,128)(2,1)}, u32[]{:S(2)}, u32[]{:S(2)}) collective-permute-start(bf16[2,256,768]{2,1,0:T(8,128)(2,1)} %get-tuple-element.32), channel_id=1, source_target_pairs={{0,1},{1,0},{2,3},{3,2},{4,5},{5,4},{6,7},{7,6},{8,9},{9,8},{10,11... | collective-permute-start | bytes 2359304 | tf_op jit(solution)/shard_map/ppermute | solution.py:357
  131.2 57.9 %collective-permute-start.9 = (bf16[2,256,768]{2,1,0:T(8,128)(2,1)}, bf16[2,256,768]{2,1,0:T(8,128)(2,1)}, u32[]{:S(2)}, u32[]{:S(2)}) collective-permute-start(bf16[2,256,768]{2,1,0:T(8,128)(2,1)} %get-tuple-element.28), channel_id=1, source_target_pairs={{0,1},{1,0},{2,3},{3,2},{4,5},{5,4},{6,7},{7,6},{8,9},{9,8},{10,11... | collective-permute-start | bytes 2359304 | tf_op jit(solution)/shard_map/ppermute | solution.py:357
  147.6 43.4 %collective-permute-start.14 = (bf16[2,256,768]{2,1,0:T(8,128)(2,1)}, bf16[2,256,768]{2,1,0:T(8,128)(2,1)}, u32[]{:S(2)}, u32[]{:S(2)}) collective-permute-start(bf16[2,256,768]{2,1,0:T(8,128)(2,1)} %get-tuple-element.34), channel_id=1, source_target_pairs={{0,1},{1,0},{2,3},{3,2},{4,5},{5,4},{6,7},{7,6},{8,9},{9,8},{10,11... | collective-permute-start | bytes 2359304 | tf_op jit(solution)/shard_map/ppermute | solution.py:357
  162.4 54.3 %collective-permute-start.50 = (bf16[688,512]{1,0:T(8,128)(2,1)}, bf16[688,512]{1,0:T(8,128)(2,1)}, u32[]{:S(2)}, u32[]{:S(2)}) collective-permute-start(bf16[688,512]{1,0:T(8,128)(2,1)} %get-tuple-element.48), channel_id=1, source_target_pairs={{0,64},{16,80},{32,96},{48,112},{64,0},{80,16},{96,32},{112,48},{1... | collective-permute-start | bytes 2113544 | tf_op jit(solution)/shard_map/ppermute | solution.py:389
  184.2 39.3 %collective-permute-start.49 = (bf16[688,512]{1,0:T(8,128)(2,1)}, bf16[688,512]{1,0:T(8,128)(2,1)S(1)}, u32[]{:S(2)}, u32[]{:S(2)}) collective-permute-start(bf16[688,512]{1,0:T(8,128)(2,1)} %get-tuple-element.46), channel_id=1, source_target_pairs={{0,64},{16,80},{32,96},{48,112},{64,0},{80,16},{96,32},{112,48},{1... | collective-permute-start | bytes 2113544 | tf_op jit(solution)/shard_map/ppermute | solution.py:388
  186.1 13.3 %collective-permute-start.39 = (bf16[688,384]{1,0:T(8,128)(2,1)S(1)}, bf16[688,384]{1,0:T(8,128)(2,1)S(1)}, u32[]{:S(2)}, u32[]{:S(2)}) collective-permute-start(bf16[688,384]{1,0:T(8,128)(2,1)S(1)} %copy-done.26), channel_id=1, source_target_pairs={{0,16},{16,32},{32,48},{48,0},{64,80},{80,96},{96,112},{112,64},{1... | collective-permute-start | bytes 1585160 | tf_op jit(solution)/shard_map/ppermute | solution.py:372
  189.1 49.8 %collective-permute-start.41 = (bf16[688,384]{1,0:T(8,128)(2,1)S(1)}, bf16[688,384]{1,0:T(8,128)(2,1)S(1)}, u32[]{:S(2)}, u32[]{:S(2)}) collective-permute-start(bf16[688,384]{1,0:T(8,128)(2,1)S(1)} %copy-done.24), channel_id=1, source_target_pairs={{0,48},{16,0},{32,16},{48,32},{64,112},{80,64},{96,80},{112,96},{1... | collective-permute-start | bytes 1585160 | tf_op jit(solution)/shard_map/ppermute | solution.py:375
  191.0 23.4 %collective-permute-start.43 = (bf16[688,384]{1,0:T(8,128)(2,1)S(1)}, bf16[688,384]{1,0:T(8,128)(2,1)S(1)}, u32[]{:S(2)}, u32[]{:S(2)}) collective-permute-start(bf16[688,384]{1,0:T(8,128)(2,1)S(1)} %copy-done.25), channel_id=1, source_target_pairs={{0,48},{16,0},{32,16},{48,32},{64,112},{80,64},{96,80},{112,96},{1... | collective-permute-start | bytes 1585160 | tf_op jit(solution)/shard_map/ppermute | solution.py:373
  199.4 29.1 %collective-permute-start.12 = (bf16[256,768]{1,0:T(8,128)(2,1)S(1)}, bf16[256,768]{1,0:T(8,128)(2,1)S(1)}, u32[]{:S(2)}, u32[]{:S(2)}) collective-permute-start(bf16[256,768]{1,0:T(8,128)(2,1)S(1)} %get-tuple-element.66), channel_id=1, source_target_pairs={{0,4},{1,5},{2,6},{3,7},{4,8},{5,9},{6,10},{7,11},{8,12},{9,13},{1... | collective-permute-start | bytes 1179656 | tf_op jit(solution)/shard_map/ppermute | solution.py:358
  216.7 13.3 %collective-permute-start.16 = (bf16[256,768]{1,0:T(8,128)(2,1)S(1)}, bf16[256,768]{1,0:T(8,128)(2,1)S(1)}, u32[]{:S(2)}, u32[]{:S(2)}) collective-permute-start(bf16[256,768]{1,0:T(8,128)(2,1)S(1)} %slice_bitcast_fusion.2), channel_id=1, source_target_pairs={{0,4},{1,5},{2,6},{3,7},{4,8},{5,9},{6,10},{7,11},{8,12},{9,13},{1... | collective-permute-start | bytes 1179656 | tf_op jit(solution)/shard_map/ppermute | solution.py:361
  223.4 15.6 %collective-permute-start.40 = (bf16[688,384]{1,0:T(8,128)(2,1)S(1)}, bf16[688,384]{1,0:T(8,128)(2,1)S(1)}, u32[]{:S(2)}, u32[]{:S(2)}) collective-permute-start(bf16[688,384]{1,0:T(8,128)(2,1)S(1)} %add_convert_fusion.5), channel_id=1, source_target_pairs={{0,16},{16,32},{32,48},{48,0},{64,80},{80,96},{96,112},{112,64},{1... | collective-permute-start | bytes 1585160 | tf_op jit(solution)/shard_map/ppermute | solution.py:376
  223.5 13.2 %collective-permute-start.18 = (bf16[256,768]{1,0:T(8,128)(2,1)S(1)}, bf16[256,768]{1,0:T(8,128)(2,1)S(1)}, u32[]{:S(2)}, u32[]{:S(2)}) collective-permute-start(bf16[256,768]{1,0:T(8,128)(2,1)S(1)} %fusion.19), channel_id=1, source_target_pairs={{0,12},{1,13},{2,14},{3,15},{4,0},{5,1},{6,2},{7,3},{8,4},{9,5},{1... | collective-permute-start | bytes 1179656 | tf_op jit(solution)/shard_map/ppermute | solution.py:363
  228.5 17.4 %collective-permute-start.42 = (bf16[688,384]{1,0:T(8,128)(2,1)S(1)}, bf16[688,384]{1,0:T(8,128)(2,1)S(1)}, u32[]{:S(2)}, u32[]{:S(2)}) collective-permute-start(bf16[688,384]{1,0:T(8,128)(2,1)S(1)} %copy-done.23), channel_id=1, source_target_pairs={{0,16},{16,32},{32,48},{48,0},{64,80},{80,96},{96,112},{112,64},{1... | collective-permute-start | bytes 1585160 | tf_op jit(solution)/shard_map/ppermute | solution.py:374
  230.0 17.3 %collective-permute-start.15 = (bf16[256,768]{1,0:T(8,128)(2,1)S(1)}, bf16[256,768]{1,0:T(8,128)(2,1)S(1)}, u32[]{:S(2)}, u32[]{:S(2)}) collective-permute-start(bf16[256,768]{1,0:T(8,128)(2,1)S(1)} %slice_bitcast_fusion.4), channel_id=1, source_target_pairs={{0,12},{1,13},{2,14},{3,15},{4,0},{5,1},{6,2},{7,3},{8,4},{9,5},{1... | collective-permute-start | bytes 1179656 | tf_op jit(solution)/shard_map/ppermute | solution.py:362
  236.7 10.4 %collective-permute-start.44 = (bf16[688,384]{1,0:T(8,128)(2,1)S(1)}, bf16[688,384]{1,0:T(8,128)(2,1)S(1)}, u32[]{:S(2)}, u32[]{:S(2)}) collective-permute-start(bf16[688,384]{1,0:T(8,128)(2,1)S(1)} %add_convert_fusion.4), channel_id=1, source_target_pairs={{0,48},{16,0},{32,16},{48,32},{64,112},{80,64},{96,80},{112,96},{1... | collective-permute-start | bytes 1585160 | tf_op jit(solution)/shard_map/ppermute | solution.py:377
  238.9 9.5 %collective-permute-start.13 = (bf16[256,768]{1,0:T(8,128)(2,1)S(1)}, bf16[256,768]{1,0:T(8,128)(2,1)S(1)}, u32[]{:S(2)}, u32[]{:S(2)}) collective-permute-start(bf16[256,768]{1,0:T(8,128)(2,1)S(1)} %fusion.22), channel_id=1, source_target_pairs={{0,4},{1,5},{2,6},{3,7},{4,8},{5,9},{6,10},{7,11},{8,12},{9,13},{1... | collective-permute-start | bytes 1179656 | tf_op jit(solution)/shard_map/ppermute | solution.py:360
  239.0 9.4 %collective-permute-start.19 = (bf16[256,768]{1,0:T(8,128)(2,1)S(1)}, bf16[256,768]{1,0:T(8,128)(2,1)S(1)}, u32[]{:S(2)}, u32[]{:S(2)}) collective-permute-start(bf16[256,768]{1,0:T(8,128)(2,1)S(1)} %fusion.21), channel_id=1, source_target_pairs={{0,2},{1,3},{2,0},{3,1},{4,6},{5,7},{6,4},{7,5},{8,10},{9,11},{10,... | collective-permute-start | bytes 1179656 | tf_op jit(solution)/shard_map/ppermute | solution.py:366
  248.6 18.4 %collective-permute-start.20 = (bf16[256,768]{1,0:T(8,128)(2,1)S(1)}, bf16[256,768]{1,0:T(8,128)(2,1)S(1)}, u32[]{:S(2)}, u32[]{:S(2)}) collective-permute-start(bf16[256,768]{1,0:T(8,128)(2,1)S(1)} %add_convert_fusion.6), channel_id=1, source_target_pairs={{0,0},{1,1},{28,2},{29,3},{40,4},{41,5},{52,6},{53,7},{2,8},{3,9},... | collective-permute-start | bytes 1179656 | tf_op jit(solution)/shard_map/ppermute | solution.py:367
  (38 other events, 608.9 us)
